TPU v7x, 1024 devices: a whole 4x8x16 slice. The times are simulated.
1024 devices in a mesh: outer: 16 (over y, core), inner: 64 (over z, x).
Axes of the slice: x: 4, y: 8, z: 16, core: 2. Of those that a mesh axis runs over, the one named last changes fastest.
Arguments:
- queries: bfloat16 [131072, 16, 128], P(('outer', 'inner')), may hold values from -160 to 160
- key_vectors: bfloat16 [131072, 128], P(('outer', 'inner')), may hold values from -6 to 6
- value_vectors: bfloat16 [131072, 128], P(('outer', 'inner')), may hold values from -6 to 6
- doc_lengths: int32 [128], replicated, may hold values from 1 to 1921, 131072 in all
Outputs:
- attended: bfloat16 [131072, 16, 128], P(('outer', 'inner'))
All inputs are finite; a program needn't handle non-finite values.
Results may differ from a plain program's by a relative error of at most 0.0037.
Values may be sent and summed in bfloat16 or wider, within the bound.
A program may use at most 32 MiB of HBM per device.

v0:
```python
import jax
import jax.numpy as jnp
from jax import lax
from jax.sharding import PartitionSpec as P

REACH = 16


def passed_along(x, axis, by):
    size = lax.axis_size(axis)
    pairs = [(i, i + by) for i in range(size) if 0 <= i + by < size]
    return lax.ppermute(x, axis, pairs)


def segment_ids(positions, starts):
    inside = (starts[None, :] <= positions[:, None]).astype(jnp.int32)
    return jnp.sum(inside, axis=1) - 1


def update(running, query_rows, key_rows, value_rows, query_seg, query_pos, key_seg, key_pos):
    row_max, row_sum, accumulated = running
    scale_factor = query_rows.shape[-1] ** (-0.5)
    scores = (
        jnp.einsum("thd,kd->thk", query_rows, key_rows, preferred_element_type=jnp.float32)
        * scale_factor
    )
    allowed = (query_seg[:, None] == key_seg[None, :]) & (key_pos[None, :] <= query_pos[:, None])
    scores = jnp.where(allowed[:, None, :], scores, -1e30)
    new_max = jnp.maximum(row_max, jnp.max(scores, axis=-1))
    rescale = jnp.exp(row_max - new_max)
    weights = jnp.exp(scores - new_max[..., None])
    row_sum = rescale * row_sum + jnp.sum(weights, axis=-1)
    rounded = weights.astype(jnp.bfloat16)
    product = jnp.einsum("thk,kd->thd", rounded, value_rows, preferred_element_type=jnp.float32)
    accumulated = rescale[..., None] * accumulated + product
    return (new_max, row_sum, accumulated)


def body(queries, key_vectors, value_vectors, doc_lengths):
    tok_rows = queries.shape[0]
    head_count = queries.shape[1]
    head_size = queries.shape[2]
    my_index = lax.axis_index(("outer", "inner"))
    starts = jnp.cumsum(doc_lengths) - doc_lengths
    offsets = jnp.arange(tok_rows, dtype=jnp.int32)
    query_pos = my_index * tok_rows + offsets
    query_seg = segment_ids(query_pos, starts)
    local_pair = (key_vectors, value_vectors)
    pieces = [local_pair]
    held_keys = key_vectors[None]
    held_values = value_vectors[None]
    distance = 1
    while distance < REACH:
        sent_count = min(distance, REACH - distance)
        arrived = passed_along((held_keys, held_values), ("outer", "inner"), distance)
        held_keys = jnp.concatenate([held_keys, arrived[0]], axis=0)
        held_values = jnp.concatenate([held_values, arrived[1]], axis=0)
        distance = distance * 2
    pieces = [(held_keys[number], held_values[number]) for number in range(REACH)]
    running = (
        jnp.full((tok_rows, head_count), -1e30, jnp.float32),
        jnp.zeros((tok_rows, head_count), jnp.float32),
        jnp.zeros((tok_rows, head_count, head_size), jnp.float32),
    )
    for distance in range(REACH - 1, -1, -1):
        key_rows, value_rows = pieces[distance]
        key_pos = (my_index - distance) * tok_rows + offsets
        key_seg = segment_ids(key_pos, starts)

        def apply_block(
            previous, key_rows=key_rows, value_rows=value_rows, key_seg=key_seg, key_pos=key_pos
        ):
            return update(
                previous, queries, key_rows, value_rows, query_seg, query_pos, key_seg, key_pos
            )

        running = apply_block(running)
    return (running[2] / running[1][..., None]).astype(jnp.bfloat16)


def solution(mesh):
    in_specs = (
        P(("outer", "inner"), None, None),
        P(("outer", "inner"), None),
        P(("outer", "inner"), None),
        P(),
    )
    out_specs = P(("outer", "inner"), None, None)
    return jax.shard_map(body, mesh=mesh, in_specs=in_specs, out_specs=out_specs, check_vma=False)
```

profile of v0, /device:TPU:48, one launch (start us, length us, event | category | flops | bytes accessed | tf_op | source)
XLA Modules:
  0.0 80.2 jit_solution(16813153753992157949)
XLA Ops:
  0.0 3.5 %collective-permute-start = (bf16[1,128,128]{2,1,0:T(8,128)(2,1)}, bf16[1,128,128]{2,1,0:T(8,128)(2,1)S(1)}, u32[]{:S(2)}, u32[]{:S(2)}) collective-permute-start(bf16[1,128,128]{2,1,0:T(8,128)(2,1)} %bitcast.221), channel_id=1, source_target_pairs={{0,1},{1,2},{2,3},{3,4},{4,5},{5,6},{6,7},{7,8},{8,9},{9,10},{10,1... | collective-permute-start | bytes 98312 | tf_op jit(solution)/shard_map/ppermute | solution.py:12
  3.5 3.4 %collective-permute-start.4 = (bf16[1,128,128]{2,1,0:T(8,128)(2,1)}, bf16[1,128,128]{2,1,0:T(8,128)(2,1)S(1)}, u32[]{:S(2)}, u32[]{:S(2)}) collective-permute-start(bf16[1,128,128]{2,1,0:T(8,128)(2,1)} %bitcast.217), channel_id=1, source_target_pairs={{0,1},{1,2},{2,3},{3,4},{4,5},{5,6},{6,7},{7,8},{8,9},{9,10},{10,1... | collective-permute-start | bytes 98312 | tf_op jit(solution)/shard_map/ppermute | solution.py:12
  7.1 0.8 copy.39
  8.2 0.7 sub.385
  9.2 0.4 compare_and_fusion.15
  9.6 0.4 copy-done.2
  10.6 12.3 %collective-permute-done = bf16[1,128,128]{2,1,0:T(8,128)(2,1)S(1)} collective-permute-done((bf16[1,128,128]{2,1,0:T(8,128)(2,1)}, bf16[1,128,128]{2,1,0:T(8,128)(2,1)S(1)}, u32[]{:S(2)}, u32[]{:S(2)}) %collective-permute-start) | collective-permute-done | bytes 32800 | tf_op jit(solution)/shard_map/ppermute | solution.py:12
  22.9 1.9 %collective-permute-start.1 = (bf16[2,128,128]{2,1,0:T(8,128)(2,1)S(1)}, bf16[2,128,128]{2,1,0:T(8,128)(2,1)S(1)}, u32[]{:S(2)}, u32[]{:S(2)}) collective-permute-start(bf16[2,128,128]{2,1,0:T(8,128)(2,1)S(1)} %pad_maximum_fusion.4), channel_id=1, source_target_pairs={{0,2},{1,3},{2,4},{3,5},{4,6},{5,7},{6,8},{7,9},{8,10},{9,11},{10,... | collective-permute-start | bytes 196616 | tf_op jit(solution)/shard_map/ppermute | solution.py:12
  24.8 1.9 %collective-permute-start.5 = (bf16[2,128,128]{2,1,0:T(8,128)(2,1)S(1)}, bf16[2,128,128]{2,1,0:T(8,128)(2,1)S(1)}, u32[]{:S(2)}, u32[]{:S(2)}) collective-permute-start(bf16[2,128,128]{2,1,0:T(8,128)(2,1)S(1)} %pad_maximum_fusion.5), channel_id=1, source_target_pairs={{0,2},{1,3},{2,4},{3,5},{4,6},{5,7},{6,8},{7,9},{8,10},{9,11},{10,... | collective-permute-start | bytes 196616 | tf_op jit(solution)/shard_map/ppermute | solution.py:12
  27.1 6.6 %collective-permute-done.1 = bf16[2,128,128]{2,1,0:T(8,128)(2,1)S(1)} collective-permute-done((bf16[2,128,128]{2,1,0:T(8,128)(2,1)S(1)}, bf16[2,128,128]{2,1,0:T(8,128)(2,1)S(1)}, u32[]{:S(2)}, u32[]{:S(2)}) %collective-permute-start.1) | collective-permute-done | bytes 65568 | tf_op jit(solution)/shard_map/ppermute | solution.py:12
  33.7 1.9 %collective-permute-start.2 = (bf16[4,128,128]{2,1,0:T(8,128)(2,1)S(1)}, bf16[4,128,128]{2,1,0:T(8,128)(2,1)S(1)}, u32[]{:S(2)}, u32[]{:S(2)}) collective-permute-start(bf16[4,128,128]{2,1,0:T(8,128)(2,1)S(1)} %pad_maximum_fusion.2), channel_id=1, source_target_pairs={{0,4},{1,5},{2,6},{3,7},{4,8},{5,9},{6,10},{7,11},{8,12},{9,13},{1... | collective-permute-start | bytes 393224 | tf_op jit(solution)/shard_map/ppermute | solution.py:12
  35.6 1.9 %collective-permute-start.6 = (bf16[4,128,128]{2,1,0:T(8,128)(2,1)S(1)}, bf16[4,128,128]{2,1,0:T(8,128)(2,1)S(1)}, u32[]{:S(2)}, u32[]{:S(2)}) collective-permute-start(bf16[4,128,128]{2,1,0:T(8,128)(2,1)S(1)} %pad_maximum_fusion.3), channel_id=1, source_target_pairs={{0,4},{1,5},{2,6},{3,7},{4,8},{5,9},{6,10},{7,11},{8,12},{9,13},{1... | collective-permute-start | bytes 393224 | tf_op jit(solution)/shard_map/ppermute | solution.py:12
  38.2 4.6 %collective-permute-done.2 = bf16[4,128,128]{2,1,0:T(8,128)(2,1)S(1)} collective-permute-done((bf16[4,128,128]{2,1,0:T(8,128)(2,1)S(1)}, bf16[4,128,128]{2,1,0:T(8,128)(2,1)S(1)}, u32[]{:S(2)}, u32[]{:S(2)}) %collective-permute-start.2) | collective-permute-done | bytes 131104 | tf_op jit(solution)/shard_map/ppermute | solution.py:12
  42.8 1.9 %collective-permute-start.3 = (bf16[8,128,128]{2,1,0:T(8,128)(2,1)S(1)}, bf16[8,128,128]{2,1,0:T(8,128)(2,1)S(1)}, u32[]{:S(2)}, u32[]{:S(2)}) collective-permute-start(bf16[8,128,128]{2,1,0:T(8,128)(2,1)S(1)} %pad_maximum_fusion), channel_id=1, source_target_pairs={{0,8},{1,9},{2,10},{3,11},{4,12},{5,13},{6,14},{7,15},{8,16},{9,17... | collective-permute-start | bytes 786440 | tf_op jit(solution)/shard_map/ppermute | solution.py:12
  44.8 0.6 collective-permute-done.6
  45.4 2.1 %collective-permute-start.7 = (bf16[8,128,128]{2,1,0:T(8,128)(2,1)S(1)}, bf16[8,128,128]{2,1,0:T(8,128)(2,1)S(1)}, u32[]{:S(2)}, u32[]{:S(2)}) collective-permute-start(bf16[8,128,128]{2,1,0:T(8,128)(2,1)S(1)} %pad_maximum_fusion.1), channel_id=1, source_target_pairs={{0,8},{1,9},{2,10},{3,11},{4,12},{5,13},{6,14},{7,15},{8,16},{9,17... | collective-permute-start | bytes 786440 | tf_op jit(solution)/shard_map/ppermute | solution.py:12
  48.8 12.7 %collective-permute-done.3 = bf16[8,128,128]{2,1,0:T(8,128)(2,1)S(1)} collective-permute-done((bf16[8,128,128]{2,1,0:T(8,128)(2,1)S(1)}, bf16[8,128,128]{2,1,0:T(8,128)(2,1)S(1)}, u32[]{:S(2)}, u32[]{:S(2)}) %collective-permute-start.3) | collective-permute-done | bytes 262176 | tf_op jit(solution)/shard_map/ppermute | solution.py:12
  68.0 0.3 fusion.100
  68.7 0.3 fusion.104
  69.4 0.3 fusion.108
  69.8 1.0 %collective-permute-done.7 = bf16[8,128,128]{2,1,0:T(8,128)(2,1)S(1)} collective-permute-done((bf16[8,128,128]{2,1,0:T(8,128)(2,1)S(1)}, bf16[8,128,128]{2,1,0:T(8,128)(2,1)S(1)}, u32[]{:S(2)}, u32[]{:S(2)}) %collective-permute-start.7) | collective-permute-done | bytes 262176 | tf_op jit(solution)/shard_map/ppermute | solution.py:12
  71.1 0.3 fusion.112
  73.2 5.8 %fusion.61 = bf16[128,16,128]{2,0,1:T(8,128)(2,1)S(1)} fusion(f32[128,16,128]{2,0,1:T(8,128)S(1)} %fusion.94, f32[128,16,128]{2,0,1:T(8,128)S(1)} %fusion.96, f32[128,16,128]{2,0,1:T(8,128)S(1)} %fusion.98, f32[128,16,128]{2,0,1:T(8,128)S(1)} %fusion.100, f32[128,16,128]{2,0,1:T(8,128)S(1)} %fusion.102, f32[128,16,128]{2,0,1:T(8,128)S(1)} %fusion.104, ...), kind=kOutput, calls=%fused_computation.78 | convolution fusion | flops 76283904 | bytes 17481728 | tf_op jit(solution)/shard_map/thk,kd->thd/dot_general | solution.py:34
  79.0 1.1 %copy.72 = bf16[128,16,128]{2,1,0:T(8,128)(2,1)} copy(bf16[128,16,128]{2,0,1:T(8,128)(2,1)S(1)} %fusion.61) | data formatting | bytes 1048576 | tf_op jit(solution)/shard_map/convert_element_type | solution.py:78
  (86 shorter events, 12.7 us)
Async XLA Ops:
  0.0 9.6 %copy-start = (bf16[128,16,128]{2,1,0:T(8,128)(2,1)S(1)}, bf16[128,16,128]{2,1,0:T(8,128)(2,1)}, u32[]{:S(2)}) copy-start(bf16[128,16,128]{2,1,0:T(8,128)(2,1)} %param.4) | copy-start | bytes 1572868
  0.0 22.8 %collective-permute-start = (bf16[1,128,128]{2,1,0:T(8,128)(2,1)}, bf16[1,128,128]{2,1,0:T(8,128)(2,1)S(1)}, u32[]{:S(2)}, u32[]{:S(2)}) collective-permute-start(bf16[1,128,128]{2,1,0:T(8,128)(2,1)} %bitcast.221), channel_id=1, source_target_pairs={{0,1},{1,2},{2,3},{3,4},{4,5},{5,6},{6,7},{7,8},{8,9},{9,10},{10,1... | collective-permute-start | bytes 98312 | tf_op jit(solution)/shard_map/ppermute | solution.py:12
  3.5 21.3 %collective-permute-start.4 = (bf16[1,128,128]{2,1,0:T(8,128)(2,1)}, bf16[1,128,128]{2,1,0:T(8,128)(2,1)S(1)}, u32[]{:S(2)}, u32[]{:S(2)}) collective-permute-start(bf16[1,128,128]{2,1,0:T(8,128)(2,1)} %bitcast.217), channel_id=1, source_target_pairs={{0,1},{1,2},{2,3},{3,4},{4,5},{5,6},{6,7},{7,8},{8,9},{9,10},{10,1... | collective-permute-start | bytes 98312 | tf_op jit(solution)/shard_map/ppermute | solution.py:12
  9.2 0.8 copy-start.2
  10.6 14.2 %copy-start.1 = (bf16[128,128]{1,0:T(8,128)(2,1)S(1)}, bf16[128,128]{1,0:T(8,128)(2,1)}, u32[]{:S(2)}) copy-start(bf16[128,128]{1,0:T(8,128)(2,1)} %param.6) | copy-start | bytes 98308
  22.9 10.8 %collective-permute-start.1 = (bf16[2,128,128]{2,1,0:T(8,128)(2,1)S(1)}, bf16[2,128,128]{2,1,0:T(8,128)(2,1)S(1)}, u32[]{:S(2)}, u32[]{:S(2)}) collective-permute-start(bf16[2,128,128]{2,1,0:T(8,128)(2,1)S(1)} %pad_maximum_fusion.4), channel_id=1, source_target_pairs={{0,2},{1,3},{2,4},{3,5},{4,6},{5,7},{6,8},{7,9},{8,10},{9,11},{10,... | collective-permute-start | bytes 196616 | tf_op jit(solution)/shard_map/ppermute | solution.py:12
  24.8 10.8 %collective-permute-start.5 = (bf16[2,128,128]{2,1,0:T(8,128)(2,1)S(1)}, bf16[2,128,128]{2,1,0:T(8,128)(2,1)S(1)}, u32[]{:S(2)}, u32[]{:S(2)}) collective-permute-start(bf16[2,128,128]{2,1,0:T(8,128)(2,1)S(1)} %pad_maximum_fusion.5), channel_id=1, source_target_pairs={{0,2},{1,3},{2,4},{3,5},{4,6},{5,7},{6,8},{7,9},{8,10},{9,11},{10,... | collective-permute-start | bytes 196616 | tf_op jit(solution)/shard_map/ppermute | solution.py:12
  33.7 9.1 %collective-permute-start.2 = (bf16[4,128,128]{2,1,0:T(8,128)(2,1)S(1)}, bf16[4,128,128]{2,1,0:T(8,128)(2,1)S(1)}, u32[]{:S(2)}, u32[]{:S(2)}) collective-permute-start(bf16[4,128,128]{2,1,0:T(8,128)(2,1)S(1)} %pad_maximum_fusion.2), channel_id=1, source_target_pairs={{0,4},{1,5},{2,6},{3,7},{4,8},{5,9},{6,10},{7,11},{8,12},{9,13},{1... | collective-permute-start | bytes 393224 | tf_op jit(solution)/shard_map/ppermute | solution.py:12
  35.6 9.7 %collective-permute-start.6 = (bf16[4,128,128]{2,1,0:T(8,128)(2,1)S(1)}, bf16[4,128,128]{2,1,0:T(8,128)(2,1)S(1)}, u32[]{:S(2)}, u32[]{:S(2)}) collective-permute-start(bf16[4,128,128]{2,1,0:T(8,128)(2,1)S(1)} %pad_maximum_fusion.3), channel_id=1, source_target_pairs={{0,4},{1,5},{2,6},{3,7},{4,8},{5,9},{6,10},{7,11},{8,12},{9,13},{1... | collective-permute-start | bytes 393224 | tf_op jit(solution)/shard_map/ppermute | solution.py:12
  42.8 18.7 %collective-permute-start.3 = (bf16[8,128,128]{2,1,0:T(8,128)(2,1)S(1)}, bf16[8,128,128]{2,1,0:T(8,128)(2,1)S(1)}, u32[]{:S(2)}, u32[]{:S(2)}) collective-permute-start(bf16[8,128,128]{2,1,0:T(8,128)(2,1)S(1)} %pad_maximum_fusion), channel_id=1, source_target_pairs={{0,8},{1,9},{2,10},{3,11},{4,12},{5,13},{6,14},{7,15},{8,16},{9,17... | collective-permute-start | bytes 786440 | tf_op jit(solution)/shard_map/ppermute | solution.py:12
  45.4 25.4 %collective-permute-start.7 = (bf16[8,128,128]{2,1,0:T(8,128)(2,1)S(1)}, bf16[8,128,128]{2,1,0:T(8,128)(2,1)S(1)}, u32[]{:S(2)}, u32[]{:S(2)}) collective-permute-start(bf16[8,128,128]{2,1,0:T(8,128)(2,1)S(1)} %pad_maximum_fusion.1), channel_id=1, source_target_pairs={{0,8},{1,9},{2,10},{3,11},{4,12},{5,13},{6,14},{7,15},{8,16},{9,17... | collective-permute-start | bytes 786440 | tf_op jit(solution)/shard_map/ppermute | solution.py:12
where the time goes:
time: 80.6 us; the launch traced here: 80.2 us
  waiting for transfers between devices  37.7 us (47%)
  starting transfers between devices  18.6 us (23%)
  matrix products  16.1 us (20%)
  other arithmetic  4.83 us (6%)
  local copies, waits for them, and re-layouts  2.27 us (3%)
    ppermute x8, waiting for transfers between devices, passed_along(): return lax.ppermute(x, axis, pairs)  37.7 us
    ppermute x8, starting transfers between devices, passed_along(): return lax.ppermute(x, axis, pairs)  18.6 us
    dot_general x16, matrix products, update(): jnp.einsum('thk,kd->thd', rounded, value_rows, preferred_element_type=jnp...  11 us
    dot_general x16, matrix products, update(): jnp.einsum('thd,kd->thk', query_rows, key_rows, preferred_element_type=jn...  5.16 us
    reduce_sum x16, other arithmetic, update(): row_sum = rescale * row_sum + jnp.sum(weights, axis=-1)  2.68 us
  transfers between devices with their start and end apart: 8, of which 6 were waited for; matrix products, arithmetic and copies ran while one was open for 17% of the time, Pallas kernels for 0%

commit v1 on v0

v1 whole, which is shorter than its diff:
```python
import jax
import jax.numpy as jnp
from jax import lax
from jax.experimental import pallas as pl
from jax.experimental.pallas import tpu as pltpu
from jax.sharding import PartitionSpec as P

MESH = pl.DeviceIdType.MESH
BLK = 128
NX = 4
NZ = 16
ROWS = 5
NEG = -1e30
TILE = 256
UNROLL = 2


def kernel(
    q_ref, k_ref, v_ref, dl_ref, o_ref,
    hold, qa, ka, acc, m_sc, l_sc, out_sc, dl_sc,
    ssem, rsem, lsem, osem,
):
    inner = lax.axis_size("inner")
    total = inner * lax.axis_size("outer")
    b = lax.axis_index("outer") * inner + lax.axis_index("inner")
    x = lax.rem(b, NX)
    r = b // NX
    z = lax.rem(r, NZ)

    def dev(dz, dx):
        x2 = lax.rem(x + dx + NX, NX)
        t = lax.rem(b - x + x2 + NX * dz + total, total)
        return (t // inner, lax.rem(t, inner))

    def slot(k, c):
        return (ROWS - 1 - k) * NX + lax.rem(x + c + NX, NX)

    sends = []

    def copy_of(h, k, c, dz, dx):
        src = slot(k, c)
        dst = src - NX * dz
        i = len(sends)
        return pltpu.make_async_remote_copy(
            src_ref=hold.at[src, h],
            dst_ref=hold.at[dst, h],
            send_sem=ssem.at[i],
            recv_sem=rsem.at[dst, h],
            device_id=dev(dz, dx),
            device_id_type=MESH,
        )

    def send(cond, h, k, c, dz, dx):
        cp = copy_of(h, k, c, dz, dx)
        sends.append((cond, cp))
        pl.when(cond)(cp.start)

    def recv(cond, h, k, c):
        sl = slot(k, c)

        def wait():
            pltpu.make_async_copy(hold.at[sl, h], hold.at[sl, h], rsem.at[sl, h]).wait()

        pl.when(cond)(wait)

    def mid(k):
        return (k >= 1) & (k <= 3)

    def has(k):
        return r >= k

    last = total // NX - 1

    def next_has(dz):
        return r + dz <= last

    bar = pltpu.get_barrier_semaphore()

    def say(dz, dx):
        pl.semaphore_signal(bar, inc=1, device_id=dev(dz, dx), device_id_type=MESH)

    say(0, 1)
    say(0, -1)
    pl.when(has(1))(lambda: say(-1, 0))
    for d in (2, 3, 4):
        pl.when((z == 0) & has(d))(lambda d=d: say(-d, 0))

    mine = slot(0, 0)
    kcp = pltpu.make_async_copy(k_ref, hold.at[mine, 0], lsem.at[0])
    vcp = pltpu.make_async_copy(v_ref, hold.at[mine, 1], lsem.at[1])
    qcp = pltpu.make_async_copy(q_ref, qa.at[:, pl.ds(0, 128)], lsem.at[2])
    dcp = pltpu.make_async_copy(dl_ref, dl_sc, lsem.at[3])
    kcp.start()
    vcp.start()
    dcp.start()
    qcp.start()

    direct = [(z == NZ - d) & next_has(d) for d in (2, 3, 4)]
    peers = 2 + next_has(1).astype(jnp.int32)
    for cond in direct:
        peers = peers + cond.astype(jnp.int32)
    pl.semaphore_wait(bar, peers)

    kcp.wait()
    vcp.wait()

    def level_one(k, h):
        right = mid(k) | ((k == 0) & (x < 3)) | ((k == 4) & (x == 3))
        left = mid(k) | ((k == 0) & (x == 0)) | ((k == 4) & (x > 0))
        send(right & has(k), h, k, 0, 0, 1)
        send(left & has(k), h, k, 0, 0, -1)

    def level_two(k):
        inside = (x == 1) | (x == 2)
        from_left = mid(k) | ((k == 0) & (x > 0)) | ((k == 4) & (x == 0))
        from_right = mid(k) | ((k == 0) & (x == 3)) | ((k == 4) & (x < 3))
        for h in (0, 1):
            recv(from_left & has(k), h, k, -1)
            recv(from_right & has(k), h, k, 1)
            both_right = (k == 0) & inside
            both_left = (k == 4) & inside
            if h == 0:
                send((mid(k) | both_right) & has(k), h, k, -1, 0, 1)
                send(both_left & has(k), h, k, 1, 0, -1)
            else:
                send((mid(k) | both_left) & has(k), h, k, 1, 0, -1)
                send(both_right & has(k), h, k, -1, 0, 1)

    def opposite(k):
        cond = mid(k) | ((k == 0) & (x >= 2)) | ((k == 4) & (x <= 1))
        for h in (0, 1):
            recv(cond & has(k), h, k, 2)

    for h in (0, 1):
        send(next_has(1), h, 0, 0, 1, 0)
        for d, cond in zip((2, 3, 4), direct):
            send(cond & ((d < 4) | (x > 0)), h, 0, 0, d, 0)
    for h in (0, 1):
        level_one(0, h)

    for k in range(1, ROWS):

        def clear(k=k):
            rows = pl.ds((ROWS - 1 - k) * NX, NX)
            hold[rows] = jnp.zeros((NX,) + hold.shape[1:], hold.dtype)

        pl.when(jnp.logical_not(has(k)))(clear)
    dcp.wait()
    lengths = dl_sc[...].astype(jnp.float32)
    ii = lax.broadcasted_iota(jnp.int32, (BLK, BLK), 0)
    jj = lax.broadcasted_iota(jnp.int32, (BLK, BLK), 1)
    starts = jnp.sum(jnp.where(jj < ii, lengths, 0.0), axis=1, keepdims=True)
    pos_q = (b * BLK + jj).astype(jnp.float32)
    low = jnp.max(jnp.where(starts <= pos_q, starts, 0.0), axis=0, keepdims=True)
    high = pos_q[0:1]
    base = (b - 15) * BLK

    def one_bias(i, carry):
        pos_k = (base + i * BLK + ii).astype(jnp.float32)
        ok = (pos_k >= low) & (pos_k <= high)
        ka[pl.ds(pl.multiple_of(i * BLK, BLK), BLK), pl.ds(128, 128)] = jnp.where(
            ok, 0.0, NEG
        ).astype(jnp.bfloat16)
        return carry

    lax.fori_loop(0, 16, one_bias, 0)

    def one_hot(i, carry):
        row = i * BLK + ii
        qa[pl.ds(pl.multiple_of(i * BLK, BLK), BLK), pl.ds(128, 128)] = jnp.where(
            row // 16 == jj, 1.0, 0.0
        ).astype(jnp.bfloat16)
        return carry

    lax.fori_loop(0, 16, one_hot, 0)

    early = jnp.minimum(z, 4)
    order = [0 * z]
    for s in range(1, 5):
        order.append(jnp.where(s <= early, s, early + 5 - s))
    for s in range(1, 5):
        k = order[s]
        exists = has(k) & ((k < 4) | (x > 0))
        for h in (0, 1):
            recv(exists, h, k, 0)
            onward = mid(k) & has(k) & next_has(1) & (z != NZ - 1)
            send(onward & ((k < 3) | (x > 0)), h, k, 0, 1, 0)
            level_one(k, h)
        level_two(order[s - 1])

    qcp.wait()
    scale = 128 ** (-0.5) * 1.4426950408889634
    outs = []

    def run(s):
        j = jnp.where(s < early, 3 - s, s - early)
        first = x + 1 + NX * j
        kbase = pl.multiple_of(j * 512, 512)
        for i in range(NX):
            ka[pl.ds(pl.multiple_of(kbase + i * BLK, BLK), BLK), pl.ds(0, 128)] = hold[first + i, 0]
        keys = ka[pl.ds(kbase, 512), :]
        values = hold[pl.ds(first, NX), 1].reshape(512, 128)

        def tile(t):
            rows = pl.ds(pl.multiple_of(t * TILE, TILE), TILE)
            sc = lax.dot_general(
                qa[rows, :], keys, (((1,), (1,)), ((), ())), preferred_element_type=jnp.float32
            )
            top = jnp.max(sc, axis=1, keepdims=True)
            if s > 0:
                m_old = m_sc[rows, 0:1]
                top = jnp.maximum(top, m_old)
            w = jnp.exp2((sc - top) * scale)
            total_w = jnp.sum(w, axis=1, keepdims=True)
            part = jnp.dot(w.astype(jnp.bfloat16), values, preferred_element_type=jnp.float32)
            if s > 0:
                alpha = jnp.exp2((m_old - top) * scale)
                total_w = total_w + alpha * l_sc[rows, 0:1]
                part = part + alpha * acc[rows, :]
            if s < 3:
                m_sc[rows, :] = jnp.broadcast_to(top, (TILE, 128))
                l_sc[rows, :] = jnp.broadcast_to(total_w, (TILE, 128))
                acc[rows, :] = part
            else:
                out_sc[rows, :] = (part / total_w).astype(jnp.bfloat16)

        def body(i, carry):
            for u in range(UNROLL):
                tile(i * UNROLL + u)
            if s == 3:
                rows = pl.ds(pl.multiple_of(i * TILE * UNROLL, TILE * UNROLL), TILE * UNROLL)
                pltpu.make_async_copy(out_sc.at[rows], o_ref.at[rows], osem.at[i]).start()
            return carry

        n = 2048 // (TILE * UNROLL)
        lax.fori_loop(0, n, body, 0)
        if s == 3:
            for i in range(n):
                rows = pl.ds(i * TILE * UNROLL, TILE * UNROLL)
                pltpu.make_async_copy(out_sc.at[rows], o_ref.at[rows], osem.at[i]).wait()

    opposite(order[0])
    opposite(order[1])
    opposite(order[2])
    run(0)
    opposite(order[3])
    run(1)
    level_two(order[4])
    opposite(order[4])
    run(2)
    run(3)
    for cond, cp in sends:
        pl.when(cond)(cp.wait_send)


def body(queries, key_vectors, value_vectors, doc_lengths):
    tok, heads, dim = queries.shape
    rows = tok * heads
    any_spec = pl.BlockSpec(memory_space=pl.ANY)
    out = pl.pallas_call(
        kernel,
        out_shape=jax.ShapeDtypeStruct((rows, dim), jnp.bfloat16),
        in_specs=[any_spec] * 4,
        out_specs=any_spec,
        scratch_shapes=[
            pltpu.VMEM((ROWS * NX, 2, BLK, dim), jnp.bfloat16),
            pltpu.VMEM((rows, 256), jnp.bfloat16),
            pltpu.VMEM((16 * BLK, 256), jnp.bfloat16),
            pltpu.VMEM((rows, 128), jnp.float32),
            pltpu.VMEM((rows, 128), jnp.float32),
            pltpu.VMEM((rows, 128), jnp.float32),
            pltpu.VMEM((rows, 128), jnp.bfloat16),
            pltpu.VMEM((1, 128), jnp.int32),
            pltpu.SemaphoreType.DMA((72,)),
            pltpu.SemaphoreType.DMA((ROWS * NX, 2)),
            pltpu.SemaphoreType.DMA((4,)),
            pltpu.SemaphoreType.DMA((16,)),
        ],
        compiler_params=pltpu.CompilerParams(collective_id=0, has_side_effects=True),
    )(queries.reshape(rows, dim), key_vectors, value_vectors, doc_lengths.reshape(1, -1))
    return out.reshape(tok, heads, dim)


def solution(mesh):
    in_specs = (
        P(("outer", "inner"), None, None),
        P(("outer", "inner"), None),
        P(("outer", "inner"), None),
        P(),
    )
    out_specs = P(("outer", "inner"), None, None)
    return jax.shard_map(body, mesh=mesh, in_specs=in_specs, out_specs=out_specs, check_vma=False)
```

time: 80.6 us -> 55.7 us (0.69)
  the two profiles are of different devices: /device:TPU:48 before, /device:TPU:168 now
where the time goes in v1:
time: 55.7 us; the launch traced here: 55.5 us
  Pallas kernels  53.6 us (96%)
  local copies, waits for them, and re-layouts  1.87 us (3%)
    pallas_call x1, Pallas kernels, body(): pl.pallas_call(kernel, out_shape=jax.ShapeDtypeStruct((rows, dim), jnp.bf...  53.6 us
    unnamed x1, local copies, waits for them, and re-layouts  1.87 us

profile of v1, /device:TPU:168, one launch (start us, length us, event | category | flops | bytes accessed | tf_op | source)
XLA Modules:
  0.0 55.5 jit_solution(13732949308660403599)
XLA Ops:
  0.0 53.6 %shard_map.46 = bf16[2048,128]{1,0:T(8,128)(2,1)} custom-call(bf16[2048,128]{1,0:T(8,128)(2,1)} %bitcast.4, bf16[128,128]{1,0:T(8,128)(2,1)} %k_ref.1, bf16[128,128]{1,0:T(8,128)(2,1)} %v_ref.1, s32[1,128]{1,0:T(1,128)} %bitcast.5), custom_call_target="tpu_custom_call" | custom-call | tf_op jit(solution)/shard_map/pallas_call | solution.py:260
  53.6 1.9 %copy.6 = bf16[128,16,128]{2,1,0:T(8,128)(2,1)} copy(bf16[128,16,128]{2,1,0:T(8,128)(2,1)} %bitcast.3) | data formatting | bytes 1048576

commit v2 on v1

v2 whole, which is shorter than its diff:
```python
import jax
import jax.numpy as jnp
from jax import lax
from jax.experimental import pallas as pl
from jax.experimental.pallas import tpu as pltpu
from jax.sharding import PartitionSpec as P

MESH = pl.DeviceIdType.MESH
BLK = 128
NX = 4
NZ = 16
ROWS = 5
NEG = -1e30
TILE = 512
NSEND = 46


def kernel(
    q_ref, k_ref, v_ref, dl_ref, o_ref,
    hold, qa, ka, acc, m_sc, l_sc, out_sc, dl_sc,
    ssem, rsem, lsem, osem,
):
    inner = lax.axis_size("inner")
    total = inner * lax.axis_size("outer")
    b = lax.axis_index("outer") * inner + lax.axis_index("inner")
    x = lax.rem(b, NX)
    r = b // NX
    z = lax.rem(r, NZ)

    def dev(dz, dx):
        x2 = lax.rem(x + dx + NX, NX)
        t = lax.rem(b - x + x2 + NX * dz + total, total)
        return (t // inner, lax.rem(t, inner))

    def slot(k, c):
        return (ROWS - 1 - k) * NX + lax.rem(x + c + NX, NX)

    sends = {}

    def copy_of(i, h, k, c, dz, dx):
        src = slot(k, c)
        dst = src - NX * dz
        return pltpu.make_async_remote_copy(
            src_ref=hold.at[src, h],
            dst_ref=hold.at[dst, h],
            send_sem=ssem.at[i],
            recv_sem=rsem.at[dst, h],
            device_id=dev(dz, dx),
            device_id_type=MESH,
        )

    def send(cond, key, h, k, c, dz, dx):
        key = key + (h,)
        i, before = sends.get(key, (len(sends), []))
        cp = copy_of(i, h, k, c, dz, dx)
        sends[key] = (i, before + [(cond, cp)])
        pl.when(cond)(cp.start)

    def recv(cond, h, k, c):
        sl = slot(k, c)

        def wait():
            pltpu.make_async_copy(hold.at[sl, h], hold.at[sl, h], rsem.at[sl, h]).wait()

        pl.when(cond)(wait)

    def mid(k):
        return (k >= 1) & (k <= 3)

    def has(k):
        return r >= k

    last = total // NX - 1

    def next_has(dz):
        return r + dz <= last

    early = jnp.minimum(z, 4)

    def row_at(i):
        return jnp.where((i <= early) | (early >= 2) | (i == 0), i, early + 5 - i)

    order = [row_at(i) for i in range(ROWS)]

    bar = pltpu.get_barrier_semaphore()

    def say(dz, dx):
        pl.semaphore_signal(bar, inc=1, device_id=dev(dz, dx), device_id_type=MESH)

    say(0, 1)
    say(0, -1)
    pl.when(has(1))(lambda: say(-1, 0))
    for d in (2, 3, 4):
        pl.when((z == 0) & has(d))(lambda d=d: say(-d, 0))
    pl.when((z == 3) & has(4))(lambda: say(-4, 0))
    pl.when((z == 2) & has(3))(lambda: say(-3, 0))

    mine = slot(0, 0)
    kcp = pltpu.make_async_copy(k_ref, hold.at[mine, 0], lsem.at[0])
    vcp = pltpu.make_async_copy(v_ref, hold.at[mine, 1], lsem.at[1])
    qcp = pltpu.make_async_copy(q_ref, qa.at[:, pl.ds(0, 128)], lsem.at[2])
    dcp = pltpu.make_async_copy(dl_ref, dl_sc, lsem.at[3])
    kcp.start()
    vcp.start()
    dcp.start()
    qcp.start()

    last_row = z == NZ - 1
    reach = jnp.where(last_row, 3, NZ - z)
    over = (z >= NZ - 4) & (r + reach <= last) & (last_row | (z > NZ - 4) | (x > 0))
    peers = 2 + next_has(1).astype(jnp.int32)
    peers = peers + ((z >= NZ - 4) & (r + reach <= last)).astype(jnp.int32)
    peers = peers + (last_row & next_has(4)).astype(jnp.int32)
    pl.semaphore_wait(bar, peers)

    kcp.wait()
    vcp.wait()

    def level_one(i, h):
        k = order[i]
        right = mid(k) | ((k == 0) & (x < 3)) | ((k == 4) & (x == 3))
        left = mid(k) | ((k == 0) & (x == 0)) | ((k == 4) & (x > 0))
        send(right & has(k), ("right", i), h, k, 0, 0, 1)
        send(left & has(k), ("left", i), h, k, 0, 0, -1)

    def level_two(i, when):
        k = order[i]
        inside = (x == 1) | (x == 2)
        from_left = when & (mid(k) | ((k == 0) & (x > 0)) | ((k == 4) & (x == 0)))
        from_right = when & (mid(k) | ((k == 0) & (x == 3)) | ((k == 4) & (x < 3)))
        onward = when & has(k) & (mid(k) | inside)
        for h in (0, 1):
            recv(from_left & has(k), h, k, -1)
            recv(from_right & has(k), h, k, 1)
            leftward = (k == 4) | ((k > 0) & (h == 1))
            step = jnp.where(leftward, -1, 1)
            send(onward, ("two", i), h, k, -step, 0, step)

    def opposite(i, when):
        k = order[i]
        cond = when & (mid(k) | ((k == 0) & (x >= 2)) | ((k == 4) & (x <= 1)))
        for h in (0, 1):
            recv(cond & has(k), h, k, 2)

    for h in (0, 1):
        send(next_has(1), ("own",), h, 0, 0, 1, 0)
    for h in (0, 1):
        send(over, ("over",), h, 0, 0, reach, 0)
        send(last_row & next_has(4) & (x > 0), ("far",), h, 0, 0, 4, 0)
    for h in (0, 1):
        level_one(0, h)

    def clear(i, carry):
        k, c = ROWS - 1 - i // NX, lax.rem(i, NX)
        unused = (r < k) | ((k == 0) & (c > x)) | ((k == 4) & ((c < x) | (x + c == 0)))

        def zero():
            hold[i] = jnp.zeros(hold.shape[1:], hold.dtype)

        pl.when(unused)(zero)
        return carry

    lax.fori_loop(0, ROWS * NX, clear, 0)
    dcp.wait()
    lengths = dl_sc[...].astype(jnp.float32)
    ii = lax.broadcasted_iota(jnp.int32, (BLK, BLK), 0)
    jj = lax.broadcasted_iota(jnp.int32, (BLK, BLK), 1)
    starts = jnp.sum(jnp.where(jj < ii, lengths, 0.0), axis=1, keepdims=True)
    pos_q = (b * BLK + jj).astype(jnp.float32)
    low = jnp.max(jnp.where(starts <= pos_q, starts, 0.0), axis=0, keepdims=True)
    high = pos_q[0:1]
    base = (r - (ROWS - 1)) * (NX * BLK)

    def one_bias(i, carry):
        pos_k = (base + i * BLK + ii).astype(jnp.float32)
        ok = (pos_k >= low) & (pos_k <= high)
        ka[pl.ds(pl.multiple_of(i * BLK, BLK), BLK), pl.ds(128, 128)] = jnp.where(
            ok, 0.0, NEG
        ).astype(jnp.bfloat16)
        return carry

    lax.fori_loop(0, ROWS * NX, one_bias, 0)

    def one_hot(i, carry):
        row = i * BLK + ii
        qa[pl.ds(pl.multiple_of(i * BLK, BLK), BLK), pl.ds(128, 128)] = jnp.where(
            row // 16 == jj, 1.0, 0.0
        ).astype(jnp.bfloat16)
        return carry

    lax.fori_loop(0, 16, one_hot, 0)
    m_sc[...] = jnp.full_like(m_sc, NEG)
    l_sc[...] = jnp.zeros_like(l_sc)
    acc[...] = jnp.zeros_like(acc)

    scale = 128 ** (-0.5) * 1.4426950408889634

    def pairs(op, parts):
        while len(parts) > 1:
            parts = [op(parts[i], parts[i + 1]) for i in range(0, len(parts), 2)]
        return parts[0]

    def run(k, last=False):
        first = (ROWS - 1 - k) * NX
        kbase = pl.multiple_of(first * BLK, NX * BLK)
        for i in range(NX):
            ka[pl.ds(pl.multiple_of(kbase + i * BLK, BLK), BLK), pl.ds(0, 128)] = hold[first + i, 0]
        keys = ka[pl.ds(kbase, NX * BLK), :]
        values = hold[pl.ds(first, NX), 1].reshape(NX * BLK, 128)
        for t in range(2048 // TILE):
            rows = pl.ds(t * TILE, TILE)
            sc = lax.dot_general(
                qa[rows, :], keys, (((1,), (1,)), ((), ())), preferred_element_type=jnp.float32
            )
            cols = [sc[:, g * 128 : (g + 1) * 128] for g in range(4)]
            top = jnp.max(pairs(jnp.maximum, cols), axis=1, keepdims=True)
            m_old = m_sc[rows, :]
            top = jnp.maximum(jnp.broadcast_to(top, (TILE, 128)), m_old)
            ws = [jnp.exp2((c - top) * scale) for c in cols]
            w = jnp.concatenate([c.astype(jnp.bfloat16) for c in ws], axis=1)
            part = jnp.dot(w, values, preferred_element_type=jnp.float32)
            alpha = jnp.exp2((m_old - top) * scale)
            total_w = pairs(jnp.add, ws) + alpha * l_sc[rows, :]
            part = part + alpha * acc[rows, :]
            if last:
                norm = jnp.sum(total_w, axis=1, keepdims=True)
                out_sc[rows, :] = (part / norm).astype(jnp.bfloat16)
                pltpu.make_async_copy(out_sc.at[rows], o_ref.at[rows], osem.at[t]).start()
            else:
                m_sc[rows, :] = top
                l_sc[rows, :] = total_w
                acc[rows, :] = part

    def runs(lo, hi):
        def one(i, carry):
            run(row_at(i))
            return carry

        lax.fori_loop(lo, hi, one, 0)

    for s in range(1, 5):
        k = order[s]
        turn = s == early + 1
        level_two(s - 1, turn)
        for i in range(s):
            opposite(i, turn)
        if s == 1:
            qcp.wait()
        runs(0, jnp.where(turn, s, 0))
        if s == 4:
            level_two(3, early == 2)
            opposite(3, early == 2)
            runs(3, jnp.where(early == 2, 4, 3))
        exists = has(k) & ((k < 4) | (x > 0))
        for h in (0, 1):
            recv(exists, h, k, 0)
            onward = mid(k) & has(k) & next_has(1) & jnp.logical_not(last_row)
            skip = ((k == 2) & (z == 1)) | ((k == 3) & ((x == 0) | (z == 2)))
            send(onward & jnp.logical_not(skip), ("on", s), h, k, 0, 1, 0)
            level_one(s, h)
        level_two(s - 1, (s <= early) | ((s > early + 1) & (s < 4)))
    level_two(3, early < 2)
    opposite(1, early == 0)
    runs(1, jnp.where(early == 0, 2, 1))
    level_two(4, early >= 0)
    for i in range(3):
        opposite(i, (early == 4) | ((i == 2) & (early < 2)))
    lo = jnp.where(early == 4, 0, jnp.where(early < 2, 2, 4))
    runs(lo, jnp.where(lo == 4, 4, 3))
    opposite(3, (early == 4) | (early < 2))
    runs(jnp.where(lo == 4, 4, 3), 4)
    opposite(4, early >= 0)
    run(order[4], last=True)
    for t in range(2048 // TILE):
        rows = pl.ds(t * TILE, TILE)
        pltpu.make_async_copy(out_sc.at[rows], o_ref.at[rows], osem.at[t]).wait()
    assert len(sends) <= NSEND
    for i, copies in sends.values():
        cond = copies[0][0]
        for other, cp in copies[1:]:
            cond = cond | other
        pl.when(cond)(copies[0][1].wait_send)


def body(queries, key_vectors, value_vectors, doc_lengths):
    tok, heads, dim = queries.shape
    rows = tok * heads
    any_spec = pl.BlockSpec(memory_space=pl.ANY)
    out = pl.pallas_call(
        kernel,
        out_shape=jax.ShapeDtypeStruct((rows, dim), jnp.bfloat16),
        in_specs=[any_spec] * 4,
        out_specs=any_spec,
        scratch_shapes=[
            pltpu.VMEM((ROWS * NX, 2, BLK, dim), jnp.bfloat16),
            pltpu.VMEM((rows, 256), jnp.bfloat16),
            pltpu.VMEM((ROWS * NX * BLK, 256), jnp.bfloat16),
            pltpu.VMEM((rows, 128), jnp.float32),
            pltpu.VMEM((rows, 128), jnp.float32),
            pltpu.VMEM((rows, 128), jnp.float32),
            pltpu.VMEM((rows, 128), jnp.bfloat16),
            pltpu.VMEM((1, 128), jnp.int32),
            pltpu.SemaphoreType.DMA((NSEND,)),
            pltpu.SemaphoreType.DMA((ROWS * NX, 2)),
            pltpu.SemaphoreType.DMA((4,)),
            pltpu.SemaphoreType.DMA((4,)),
        ],
        compiler_params=pltpu.CompilerParams(collective_id=0, has_side_effects=True),
    )(queries.reshape(rows, dim), key_vectors, value_vectors, doc_lengths.reshape(1, -1))
    return out.reshape(tok, heads, dim)


def solution(mesh):
    in_specs = (
        P(("outer", "inner"), None, None),
        P(("outer", "inner"), None),
        P(("outer", "inner"), None),
        P(),
    )
    out_specs = P(("outer", "inner"), None, None)
    return jax.shard_map(body, mesh=mesh, in_specs=in_specs, out_specs=out_specs, check_vma=False)
```

time: 55.7 us -> 45.7 us (0.82)
  the two profiles are of different devices: /device:TPU:168 before, /device:TPU:178 now
where the time goes in v2:
time: 45.7 us; the launch traced here: 45.5 us
  Pallas kernels  43.6 us (95%)
  local copies, waits for them, and re-layouts  1.87 us (4%)
    pallas_call x1, Pallas kernels, body(): pl.pallas_call(kernel, out_shape=jax.ShapeDtypeStruct((rows, dim), jnp.bf...  43.6 us
    unnamed x1, local copies, waits for them, and re-layouts  1.87 us

profile of v2, /device:TPU:178, one launch (start us, length us, event | category | flops | bytes accessed | tf_op | source)
XLA Modules:
  0.0 45.5 jit_solution(6210244580271940090)
XLA Ops:
  0.0 43.6 %shard_map.46 = bf16[2048,128]{1,0:T(8,128)(2,1)} custom-call(bf16[2048,128]{1,0:T(8,128)(2,1)} %bitcast.4, bf16[128,128]{1,0:T(8,128)(2,1)} %k_ref.1, bf16[128,128]{1,0:T(8,128)(2,1)} %v_ref.1, s32[1,128]{1,0:T(1,128)} %bitcast.5), custom_call_target="tpu_custom_call" | custom-call | tf_op jit(solution)/shard_map/pallas_call | solution.py:289
  43.6 1.9 %copy.6 = bf16[128,16,128]{2,1,0:T(8,128)(2,1)} copy(bf16[128,16,128]{2,1,0:T(8,128)(2,1)} %bitcast.3) | data formatting | bytes 1048576

commit v3 on v2

--- a/solution.py
+++ b/solution.py
@@ -11,8 +11,8 @@
 NZ = 16
 ROWS = 5
 NEG = -1e30
-TILE = 512
-NSEND = 46
+TILE = 256
+NSEND = 42
 
 
 def kernel(
@@ -78,7 +78,7 @@
     early = jnp.minimum(z, 4)
 
     def row_at(i):
-        return jnp.where((i <= early) | (early >= 2) | (i == 0), i, early + 5 - i)
+        return jnp.where((i <= early) | (i == 0), i, early + 5 - i)
 
     order = [row_at(i) for i in range(ROWS)]
 
@@ -93,7 +93,6 @@
     for d in (2, 3, 4):
         pl.when((z == 0) & has(d))(lambda d=d: say(-d, 0))
     pl.when((z == 3) & has(4))(lambda: say(-4, 0))
-    pl.when((z == 2) & has(3))(lambda: say(-3, 0))
 
     mine = slot(0, 0)
     kcp = pltpu.make_async_copy(k_ref, hold.at[mine, 0], lsem.at[0])
@@ -106,11 +105,10 @@
     qcp.start()
 
     last_row = z == NZ - 1
-    reach = jnp.where(last_row, 3, NZ - z)
-    over = (z >= NZ - 4) & (r + reach <= last) & (last_row | (z > NZ - 4) | (x > 0))
-    peers = 2 + next_has(1).astype(jnp.int32)
-    peers = peers + ((z >= NZ - 4) & (r + reach <= last)).astype(jnp.int32)
-    peers = peers + (last_row & next_has(4)).astype(jnp.int32)
+    reach = jnp.where(last_row, 4, NZ - z)
+    afar = (z >= NZ - 4) & (r + reach <= last)
+    over = afar & ((x > 0) | (reach < 4))
+    peers = 2 + next_has(1).astype(jnp.int32) + afar.astype(jnp.int32)
     pl.semaphore_wait(bar, peers)
 
     kcp.wait()
@@ -143,10 +141,11 @@
             recv(cond & has(k), h, k, 2)
 
     for h in (0, 1):
+        send(over & jnp.logical_not(last_row), ("over",), h, 0, 0, reach, 0)
+    for h in (0, 1):
         send(next_has(1), ("own",), h, 0, 0, 1, 0)
     for h in (0, 1):
-        send(over, ("over",), h, 0, 0, reach, 0)
-        send(last_row & next_has(4) & (x > 0), ("far",), h, 0, 0, 4, 0)
+        send(over & last_row, ("over",), h, 0, 0, reach, 0)
     for h in (0, 1):
         level_one(0, h)
 
@@ -174,7 +173,9 @@
     def one_bias(i, carry):
         pos_k = (base + i * BLK + ii).astype(jnp.float32)
         ok = (pos_k >= low) & (pos_k <= high)
-        ka[pl.ds(pl.multiple_of(i * BLK, BLK), BLK), pl.ds(128, 128)] = jnp.where(
+        row, col = i // NX, lax.rem(i, NX)
+        place = jnp.where(row == ROWS - 1, col, NX + col * NX + row)
+        ka[pl.ds(pl.multiple_of(place * BLK, BLK), BLK), pl.ds(128, 128)] = jnp.where(
             ok, 0.0, NEG
         ).astype(jnp.bfloat16)
         return carry
@@ -200,86 +201,99 @@
             parts = [op(parts[i], parts[i + 1]) for i in range(0, len(parts), 2)]
         return parts[0]
 
-    def run(k, last=False):
-        first = (ROWS - 1 - k) * NX
-        kbase = pl.multiple_of(first * BLK, NX * BLK)
+    def run(unit, last=False):
+        first = jnp.where(unit == 0, (ROWS - 1) * NX, unit - 1)
+        step = jnp.where(unit == 0, 1, NX)
+        kbase = pl.multiple_of(unit * (NX * BLK), NX * BLK)
         for i in range(NX):
-            ka[pl.ds(pl.multiple_of(kbase + i * BLK, BLK), BLK), pl.ds(0, 128)] = hold[first + i, 0]
+            at = pl.ds(pl.multiple_of(kbase + i * BLK, BLK), BLK)
+            ka[at, pl.ds(0, 128)] = hold[first + step * i, 0]
         keys = ka[pl.ds(kbase, NX * BLK), :]
-        values = hold[pl.ds(first, NX), 1].reshape(NX * BLK, 128)
-        for t in range(2048 // TILE):
+        values = jnp.concatenate([hold[first + step * i, 1] for i in range(NX)], axis=0)
+
+        def score(t):
+            return lax.dot_general(
+                qa[pl.ds(t * TILE, TILE), :],
+                keys,
+                (((1,), (1,)), ((), ())),
+                preferred_element_type=jnp.float32,
+            )
+
+        def weigh(t, sc):
             rows = pl.ds(t * TILE, TILE)
-            sc = lax.dot_general(
-                qa[rows, :], keys, (((1,), (1,)), ((), ())), preferred_element_type=jnp.float32
-            )
             cols = [sc[:, g * 128 : (g + 1) * 128] for g in range(4)]
             top = jnp.max(pairs(jnp.maximum, cols), axis=1, keepdims=True)
             m_old = m_sc[rows, :]
             top = jnp.maximum(jnp.broadcast_to(top, (TILE, 128)), m_old)
             ws = [jnp.exp2((c - top) * scale) for c in cols]
-            w = jnp.concatenate([c.astype(jnp.bfloat16) for c in ws], axis=1)
-            part = jnp.dot(w, values, preferred_element_type=jnp.float32)
             alpha = jnp.exp2((m_old - top) * scale)
-            total_w = pairs(jnp.add, ws) + alpha * l_sc[rows, :]
-            part = part + alpha * acc[rows, :]
+            m_sc[rows, :] = top
+            l_sc[rows, :] = pairs(jnp.add, ws) + alpha * l_sc[rows, :]
+            return jnp.concatenate([c.astype(jnp.bfloat16) for c in ws], axis=1), alpha
+
+        def add(t, w, alpha):
+            rows = pl.ds(t * TILE, TILE)
+            part = jnp.dot(w, values, preferred_element_type=jnp.float32) + alpha * acc[rows, :]
             if last:
-                norm = jnp.sum(total_w, axis=1, keepdims=True)
+                norm = jnp.sum(l_sc[rows, :], axis=1, keepdims=True)
                 out_sc[rows, :] = (part / norm).astype(jnp.bfloat16)
                 pltpu.make_async_copy(out_sc.at[rows], o_ref.at[rows], osem.at[t]).start()
             else:
-                m_sc[rows, :] = top
-                l_sc[rows, :] = total_w
                 acc[rows, :] = part
 
-    def runs(lo, hi):
-        def one(i, carry):
-            run(row_at(i))
-            return carry
-
-        lax.fori_loop(lo, hi, one, 0)
-
+        n = 2048 // TILE
+        scores, weights = {}, {}
+        for u in range(n + 2):
+            if u < n:
+                scores[u] = score(u)
+            if 0 <= u - 1 < n:
+                weights[u - 1] = weigh(u - 1, scores.pop(u - 1))
+            if 0 <= u - 2:
+                add(u - 2, *weights.pop(u - 2))
+
+    def column(c):
+        return 1 + lax.rem(x + c + NX, NX)
+
+    level_two(0, early >= 0)
+    opposite(0, early >= 0)
+    qcp.wait()
+    run(0 * z)
     for s in range(1, 5):
         k = order[s]
-        turn = s == early + 1
-        level_two(s - 1, turn)
-        for i in range(s):
-            opposite(i, turn)
-        if s == 1:
-            qcp.wait()
-        runs(0, jnp.where(turn, s, 0))
-        if s == 4:
-            level_two(3, early == 2)
-            opposite(3, early == 2)
-            runs(3, jnp.where(early == 2, 4, 3))
+        if s > 1:
+            level_two(s - 1, s == early + 1)
         exists = has(k) & ((k < 4) | (x > 0))
         for h in (0, 1):
             recv(exists, h, k, 0)
             onward = mid(k) & has(k) & next_has(1) & jnp.logical_not(last_row)
-            skip = ((k == 2) & (z == 1)) | ((k == 3) & ((x == 0) | (z == 2)))
+            skip = (k == 3) & ((x == 0) | (z == 2))
             send(onward & jnp.logical_not(skip), ("on", s), h, k, 0, 1, 0)
             level_one(s, h)
-        level_two(s - 1, (s <= early) | ((s > early + 1) & (s < 4)))
-    level_two(3, early < 2)
-    opposite(1, early == 0)
-    runs(1, jnp.where(early == 0, 2, 1))
+        if s > 1:
+            level_two(s - 1, s <= early)
+    for i in (1, 2):
+        level_two(i, i > early)
+    run(column(0))
+    level_two(3, early < 3)
     level_two(4, early >= 0)
-    for i in range(3):
-        opposite(i, (early == 4) | ((i == 2) & (early < 2)))
-    lo = jnp.where(early == 4, 0, jnp.where(early < 2, 2, 4))
-    runs(lo, jnp.where(lo == 4, 4, 3))
-    opposite(3, (early == 4) | (early < 2))
-    runs(jnp.where(lo == 4, 4, 3), 4)
-    opposite(4, early >= 0)
-    run(order[4], last=True)
-    for t in range(2048 // TILE):
-        rows = pl.ds(t * TILE, TILE)
-        pltpu.make_async_copy(out_sc.at[rows], o_ref.at[rows], osem.at[t]).wait()
+
+    def side(i, carry):
+        run(column(2 * i - 1))
+        return carry
+
+    lax.fori_loop(0, 2, side, 0)
+    for i in range(1, ROWS):
+        opposite(i, early >= 0)
+    run(column(2), last=True)
     assert len(sends) <= NSEND
     for i, copies in sends.values():
         cond = copies[0][0]
         for other, cp in copies[1:]:
             cond = cond | other
         pl.when(cond)(copies[0][1].wait_send)
+    for t in range(2048 // TILE):
+        rows = pl.ds(t * TILE, TILE)
+        pltpu.make_async_copy(out_sc.at[rows], o_ref.at[rows], osem.at[t]).wait()
 
 
 def body(queries, key_vectors, value_vectors, doc_lengths):
@@ -303,7 +317,7 @@
             pltpu.SemaphoreType.DMA((NSEND,)),
             pltpu.SemaphoreType.DMA((ROWS * NX, 2)),
             pltpu.SemaphoreType.DMA((4,)),
-            pltpu.SemaphoreType.DMA((4,)),
+            pltpu.SemaphoreType.DMA((2048 // TILE,)),
         ],
         compiler_params=pltpu.CompilerParams(collective_id=0, has_side_effects=True),
     )(queries.reshape(rows, dim), key_vectors, value_vectors, doc_lengths.reshape(1, -1))

time: 45.7 us -> 42.8 us (0.937)
  the two profiles are of different devices: /device:TPU:178 before, /device:TPU:176 now
where the time goes in v3:
time: 42.8 us; the launch traced here: 42.6 us
  Pallas kernels  40.7 us (95%)
  local copies, waits for them, and re-layouts  1.87 us (4%)
    pallas_call x1, Pallas kernels, body(): pl.pallas_call(kernel, out_shape=jax.ShapeDtypeStruct((rows, dim), jnp.bf...  40.7 us
    unnamed x1, local copies, waits for them, and re-layouts  1.87 us

profile of v3, /device:TPU:176, one launch (start us, length us, event | category | flops | bytes accessed | tf_op | source)
XLA Modules:
  0.0 42.6 jit_solution(5835785947981641702)
XLA Ops:
  0.0 40.7 %shard_map.46 = bf16[2048,128]{1,0:T(8,128)(2,1)} custom-call(bf16[2048,128]{1,0:T(8,128)(2,1)} %bitcast.4, bf16[128,128]{1,0:T(8,128)(2,1)} %k_ref.1, bf16[128,128]{1,0:T(8,128)(2,1)} %v_ref.1, s32[1,128]{1,0:T(1,128)} %bitcast.5), custom_call_target="tpu_custom_call" | custom-call | tf_op jit(solution)/shard_map/pallas_call | solution.py:303
  40.7 1.9 %copy.6 = bf16[128,16,128]{2,1,0:T(8,128)(2,1)} copy(bf16[128,16,128]{2,1,0:T(8,128)(2,1)} %bitcast.3) | data formatting | bytes 1048576

commit v4 on v3

--- a/solution.py
+++ b/solution.py
@@ -81,6 +81,16 @@
         return jnp.where((i <= early) | (i == 0), i, early + 5 - i)
 
     order = [row_at(i) for i in range(ROWS)]
+
+    late = 4 - early
+
+    def slot_of(n):
+        m = n - NX * (early + 1)
+        turn = sum((m >= late * t).astype(jnp.int32) for t in (1, 2, 3))
+        shift = jnp.where(turn == 0, 0, jnp.where(turn == 1, NX - 1, turn - 1))
+        late_slot = (m - turn * late) * NX + lax.rem(x + shift, NX)
+        early_slot = (ROWS - 1 - n // NX) * NX + lax.rem(n, NX)
+        return jnp.where(m < 0, early_slot, late_slot)
 
     bar = pltpu.get_barrier_semaphore()
 
@@ -171,11 +181,9 @@
     base = (r - (ROWS - 1)) * (NX * BLK)
 
     def one_bias(i, carry):
-        pos_k = (base + i * BLK + ii).astype(jnp.float32)
+        pos_k = (base + slot_of(i) * BLK + ii).astype(jnp.float32)
         ok = (pos_k >= low) & (pos_k <= high)
-        row, col = i // NX, lax.rem(i, NX)
-        place = jnp.where(row == ROWS - 1, col, NX + col * NX + row)
-        ka[pl.ds(pl.multiple_of(place * BLK, BLK), BLK), pl.ds(128, 128)] = jnp.where(
+        ka[pl.ds(pl.multiple_of(i * BLK, BLK), BLK), pl.ds(128, 128)] = jnp.where(
             ok, 0.0, NEG
         ).astype(jnp.bfloat16)
         return carry
@@ -202,14 +210,13 @@
         return parts[0]
 
     def run(unit, last=False):
-        first = jnp.where(unit == 0, (ROWS - 1) * NX, unit - 1)
-        step = jnp.where(unit == 0, 1, NX)
+        slots = [slot_of(unit * NX + i) for i in range(NX)]
         kbase = pl.multiple_of(unit * (NX * BLK), NX * BLK)
         for i in range(NX):
             at = pl.ds(pl.multiple_of(kbase + i * BLK, BLK), BLK)
-            ka[at, pl.ds(0, 128)] = hold[first + step * i, 0]
+            ka[at, pl.ds(0, 128)] = hold[slots[i], 0]
         keys = ka[pl.ds(kbase, NX * BLK), :]
-        values = jnp.concatenate([hold[first + step * i, 1] for i in range(NX)], axis=0)
+        values = jnp.concatenate([hold[slots[i], 1] for i in range(NX)], axis=0)
 
         def score(t):
             return lax.dot_general(
@@ -251,8 +258,12 @@
             if 0 <= u - 2:
                 add(u - 2, *weights.pop(u - 2))
 
-    def column(c):
-        return 1 + lax.rem(x + c + NX, NX)
+    def runs(lo, hi):
+        def one(i, carry):
+            run(i)
+            return carry
+
+        lax.fori_loop(lo, hi, one, 0)
 
     level_two(0, early >= 0)
     opposite(0, early >= 0)
@@ -261,7 +272,11 @@
     for s in range(1, 5):
         k = order[s]
         if s > 1:
-            level_two(s - 1, s == early + 1)
+            turn = s == early + 1
+            level_two(s - 1, turn)
+            for i in range(1, s):
+                opposite(i, turn)
+            runs(1, jnp.where(turn, s, 1))
         exists = has(k) & ((k < 4) | (x > 0))
         for h in (0, 1):
             recv(exists, h, k, 0)
@@ -273,18 +288,15 @@
             level_two(s - 1, s <= early)
     for i in (1, 2):
         level_two(i, i > early)
-    run(column(0))
+    runs(early + 1, jnp.where(early < 2, early + 2, early + 1))
     level_two(3, early < 3)
     level_two(4, early >= 0)
-
-    def side(i, carry):
-        run(column(2 * i - 1))
-        return carry
-
-    lax.fori_loop(0, 2, side, 0)
     for i in range(1, ROWS):
-        opposite(i, early >= 0)
-    run(column(2), last=True)
+        opposite(i, early == 4)
+    runs(jnp.where(early == 4, 1, jnp.where(early == 3, 4, jnp.where(early == 0, 2, 3))), 4)
+    for i in range(1, ROWS):
+        opposite(i, i > early)
+    run(4 + 0 * z, last=True)
     assert len(sends) <= NSEND
     for i, copies in sends.values():
         cond = copies[0][0]

time: 42.8 us -> 42 us (0.981)
  Pallas kernels: 40.7 us -> 39.9 us
    pallas_call x1, Pallas kernels: 40.7 us -> 39.9 us  [body(): pl.pallas_call(kernel, out_shape=jax.ShapeDtypeStruct((rows, dim), jnp.bf...]
where the time goes in v4:
time: 42 us; the launch traced here: 41.8 us
  Pallas kernels  39.9 us (95%)
  local copies, waits for them, and re-layouts  1.87 us (4%)
    pallas_call x1, Pallas kernels, body(): pl.pallas_call(kernel, out_shape=jax.ShapeDtypeStruct((rows, dim), jnp.bf...  39.9 us
    unnamed x1, local copies, waits for them, and re-layouts  1.87 us

profile of v4, /device:TPU:176, one launch (start us, length us, event | category | flops | bytes accessed | tf_op | source)
XLA Modules:
  0.0 41.8 jit_solution(2338289129358111666)
XLA Ops:
  0.0 39.9 %shard_map.46 = bf16[2048,128]{1,0:T(8,128)(2,1)} custom-call(bf16[2048,128]{1,0:T(8,128)(2,1)} %bitcast.4, bf16[128,128]{1,0:T(8,128)(2,1)} %k_ref.1, bf16[128,128]{1,0:T(8,128)(2,1)} %v_ref.1, s32[1,128]{1,0:T(1,128)} %bitcast.5), custom_call_target="tpu_custom_call" | custom-call | tf_op jit(solution)/shard_map/pallas_call | solution.py:315
  39.9 1.9 %copy.6 = bf16[128,16,128]{2,1,0:T(8,128)(2,1)} copy(bf16[128,16,128]{2,1,0:T(8,128)(2,1)} %bitcast.3) | data formatting | bytes 1048576
